TPU v7x, 32 devices: a whole 2x2x4 slice. The times are simulated.
32 devices in a mesh: row: 4 (over y, x), col: 8 (over z, core).
Axes of the slice: x: 2, y: 2, z: 4, core: 2. Of those that a mesh axis runs over, the one named last changes fastest.
Arguments:
- patches: bfloat16 [32, 128, 768], P('row', 'col'), may hold values from -6 to 6
- w_patch: bfloat16 [768, 6144], replicated, may hold values from -0.21875 to 0.21875
- patch_bias: bfloat16 [6144], replicated, may hold values from -5 to 5
- ln_gain: bfloat16 [6144], replicated, may hold values from 0.5 to 1.5
- w_qkv: bfloat16 [6144, 3, 48, 128], P(None, None, 'col'), may hold values from -1 to 1
- qk_gain: float32 [2, 48, 128], P(None, 'col'), may hold values from 0 to 6, as said below
- w_out: bfloat16 [48, 128, 6144], P('col', None, 'row'), may hold values from -0.078125 to 0.078125
Outputs:
- attn_branch: bfloat16 [4096, 6144], P(('row', 'col'))
Inputs may be any that keep to these rules, and one draw needn't show every extreme that they name: `qk_gain`: positive gains.
All inputs are finite; a program needn't handle non-finite values.
Results may differ from a plain program's by a relative error of at most 0.015.
Values may be sent and summed in bfloat16 or wider, within the bound.
A program may use at most 320 MiB of HBM per device.

v0:
```python
import math

import jax
import jax.numpy as jnp
from jax import lax
from jax.sharding import PartitionSpec as P

NORM_EPS = 1e-06


def sincos_table(row_ids, col_ids, model_width):
    quarter = model_width // 4
    frequency = 1.0 / 10000.0 ** (jnp.arange(quarter, dtype=jnp.float32) / quarter)
    row_angle = row_ids.astype(jnp.float32)[:, None] * frequency[None, :]
    col_angle = col_ids.astype(jnp.float32)[:, None] * frequency[None, :]
    return jnp.concatenate(
        [jnp.sin(row_angle), jnp.cos(row_angle), jnp.sin(col_angle), jnp.cos(col_angle)], axis=1
    )


def layer_norm(values, gain_row):
    mean_val = jnp.mean(values, axis=-1, keepdims=True)
    centered = values - mean_val
    variance = jnp.mean(centered * centered, axis=-1, keepdims=True)
    return centered * lax.rsqrt(variance + NORM_EPS) * gain_row


def local(patches, w_patch, patch_bias, ln_gain, w_qkv, qk_gain, w_out):
    tile_rows, tile_cols, pixel_width = patches.shape
    model_width = w_patch.shape[1]
    heads_here = w_qkv.shape[2]
    head_size = w_qkv.shape[3]
    col_count = lax.axis_size("col")
    block_tokens = tile_rows * tile_cols * col_count
    row_anchor = lax.axis_index("row") * tile_rows
    qkv_matrix = w_qkv.reshape(model_width, 3 * heads_here * head_size)
    bias_row = patch_bias.astype(jnp.float32)[None, :]
    gain_row = ln_gain.astype(jnp.float32)
    pixels = lax.all_gather(patches, "col", axis=1, tiled=True)
    piece_cols = pixels.shape[1]
    local_rows = jnp.repeat(jnp.arange(tile_rows, dtype=jnp.int32), piece_cols)
    local_cols = jnp.tile(jnp.arange(piece_cols, dtype=jnp.int32), tile_rows)
    flat_pixels = pixels.reshape(tile_rows * piece_cols, pixel_width)
    embedded = jnp.dot(flat_pixels, w_patch, preferred_element_type=jnp.float32) + bias_row
    embedded = embedded + sincos_table(row_anchor + local_rows, local_cols, model_width)
    normed = layer_norm(embedded, gain_row).astype(jnp.bfloat16)
    normed_piece = normed.reshape(tile_rows, piece_cols, model_width)
    project_piece_cols = normed_piece.shape[1]
    flat_normed = normed_piece.reshape(tile_rows * project_piece_cols, model_width)
    projected = jnp.dot(flat_normed, qkv_matrix, preferred_element_type=jnp.float32)
    projected = projected.reshape(tile_rows, project_piece_cols, 3 * heads_here * head_size)
    projected = projected.reshape(block_tokens, 3, heads_here, head_size)
    queries = layer_norm(projected[:, 0], qk_gain[0]).astype(jnp.bfloat16)
    keys_here = layer_norm(projected[:, 1], qk_gain[1]).astype(jnp.bfloat16)
    values_here = projected[:, 2].astype(jnp.bfloat16)
    query_heads = queries.transpose(1, 0, 2)
    scale_factor = 1.0 / math.sqrt(head_size)
    start_state = (
        jnp.full((heads_here, block_tokens), -1e30, jnp.float32),
        jnp.zeros((heads_here, block_tokens), jnp.float32),
        jnp.zeros((heads_here, block_tokens, head_size), jnp.float32),
    )
    key_piece = lax.all_gather(keys_here, "row", axis=0, tiled=True)
    value_piece = lax.all_gather(values_here, "row", axis=0, tiled=True)
    piece_len = key_piece.shape[0]
    key_block = math.gcd(piece_len, 1024)
    block_count = piece_len // key_block
    key_blocks = key_piece.reshape(block_count, key_block, heads_here, head_size)
    value_blocks = value_piece.reshape(block_count, key_block, heads_here, head_size)

    def step_block(state, block_args):
        run_peak, run_total, run_acc = state
        block_keys, block_values = block_args
        scores = (
            jnp.einsum("hqd,khd->hqk", query_heads, block_keys, preferred_element_type=jnp.float32)
            * scale_factor
        )
        new_peak = jnp.maximum(run_peak, jnp.max(scores, axis=2))
        rescale = jnp.exp(run_peak - new_peak)
        exponent = jnp.exp(scores - new_peak[:, :, None])
        new_total = run_total * rescale + jnp.sum(exponent, axis=2)
        weighted = jnp.einsum(
            "hqk,khd->hqd",
            exponent.astype(jnp.bfloat16),
            block_values,
            preferred_element_type=jnp.float32,
        )
        new_acc = run_acc * rescale[:, :, None] + weighted
        return ((new_peak, new_total, new_acc), None)

    final_state, unused = lax.scan(step_block, start_state, (key_blocks, value_blocks))
    peak_all, total_all, acc_all = final_state
    context = (acc_all / total_all[:, :, None]).astype(jnp.bfloat16)
    context = context.transpose(1, 0, 2).reshape(block_tokens, heads_here * head_size)
    out_weight = lax.all_gather(w_out, "row", axis=2, tiled=True).reshape(
        heads_here * head_size, model_width
    )
    return lax.psum_scatter(
        jnp.dot(context, out_weight, preferred_element_type=jnp.float32).astype(jnp.bfloat16),
        "col",
        scatter_dimension=0,
        tiled=True,
    )


def solution(mesh):
    return jax.shard_map(
        local,
        mesh=mesh,
        in_specs=(
            P("row", "col", None),
            P(),
            P(),
            P(),
            P(None, None, "col", None),
            P(None, "col", None),
            P("col", None, "row"),
        ),
        out_specs=P(("row", "col"), None),
        check_vma=False,
    )
```

profile of v0, /device:TPU:0, one launch (start us, length us, event | category | flops | bytes accessed | tf_op | source)
XLA Modules:
  0.0 631.0 jit_solution(16349719539641851866)
XLA Ops:
  8.0 36.8 %copy.13 = bf16[6144,3,6,128]{0,3,2,1:T(8,128)(2,1)} copy(bf16[6144,3,6,128]{3,0,2,1:T(8,128)(2,1)} %param.13) | data formatting | bytes 56623104 | tf_op args[4]
  44.9 46.9 %multiply_sine_fusion.1 = (f32[1024,1536]{1,0:T(8,128)}, f32[1024,1536]{1,0:T(8,128)}, f32[1024,1536]{1,0:T(8,128)}, f32[1024,1536]{1,0:T(8,128)}) fusion(f32[1536]{0:T(1024)S(1)} %negate_power_fusion, f32[1024]{0:T(1024)S(1)} %get-tuple-element.118, f32[1024]{0:T(1024)S(1)} %get-tuple-element.117), kind=kLoop, calls=%fused_computation.35 | loop fusion | flops 3145728 | bytes 25180160 | tf_op jit(solution)/shard_map/sin | solution.py:17
  91.8 24.2 %fusion.29 = (f32[1024]{0:T(1024)S(1)}, f32[1024,6144]{1,0:T(8,128)}) fusion(f32[1024,1536]{1,0:T(8,128)} %get-tuple-element.111, f32[1024,1536]{1,0:T(8,128)} %get-tuple-element.112, f32[1024,1536]{1,0:T(8,128)} %get-tuple-element.108, f32[1024,1536]{1,0:T(8,128)} %get-tuple-element.107, f32[6144]{0:T(1024)S(1)} %convert_element_type.52, ...), kind=kOutput, calls=%fused_computation.60 | convolution fusion | flops 9701424128 | bytes 61370368 | tf_op jit(solution)/shard_map/dot_general | solution.py:44
  126.2 36.4 %fusion.19 = f32[1024,3,6,128]{0,3,2,1:T(8,128)S(1)} fusion(bf16[6144,3,6,128]{0,3,2,1:T(8,128)(2,1)} %copy.13, f32[1024,6144]{1,0:T(8,128)} %get-tuple-element.116, f32[6144]{0:T(1024)S(1)} %convert_element_type.57, f32[1024]{0:T(1024)S(1)} %add_rsqrt_fusion.2, f32[1024]{0:T(1024)S(1)} %broadcast_multiply_fusion.2), kind=kOutput, calls=%fused_computation.22 | convolution fusion | flops 29016195072 | bytes 62947328 | tf_op jit(solution)/shard_map/dot_general | solution.py:50
  173.3 67.7 %all-gather.8.cloned.1.call-done = bf16[4096,6,128]{0,2,1:T(8,128)(2,1)} async-done(((bf16[1024,6,128]{0,2,1:T(8,128)(2,1)}), bf16[4096,6,128]{0,2,1:T(8,128)(2,1)}) %all-gather.8.cloned.1.call-update) | async-done | bytes 6291472 | tf_op jit(solution)/shard_map/all_gather | solution.py:63
  241.0 11.3 %reshape.81 = bf16[4,1024,6,128]{1,0,3,2:T(4,128)(2,1)} reshape(bf16[4096,6,128]{0,2,1:T(8,128)(2,1)} %all-gather.8.cloned.1.call-done) | data formatting | bytes 12582912 | tf_op jit(solution)/shard_map/reshape | solution.py:68
  252.4 11.4 %copy.16 = bf16[4,1024,6,128]{3,1,2,0:T(8,128)(2,1)} copy(bf16[4,1024,6,128]{1,0,3,2:T(4,128)(2,1)} %reshape.81) | data formatting | bytes 12582912
  263.7 49.2 %all-gather.12.cloned.1.call-done = bf16[4096,1,6,128]{0,3,2,1:T(8,128)(2,1)} async-done(((bf16[1024,1,6,128]{0,3,2,1:T(8,128)(2,1)}), bf16[4096,1,6,128]{0,3,2,1:T(8,128)(2,1)}) %all-gather.12.cloned.1.call-update) | async-done | bytes 6291472 | tf_op jit(solution)/shard_map/all_gather | solution.py:64
  313.0 11.4 %reshape.82 = bf16[4,1024,6,128]{1,0,3,2:T(4,128)(2,1)} reshape(bf16[4096,1,6,128]{0,3,2,1:T(8,128)(2,1)} %all-gather.12.cloned.1.call-done) | data formatting | bytes 12582912 | tf_op jit(solution)/shard_map/reshape | solution.py:69
  324.4 11.3 %copy.18 = bf16[4,1024,6,128]{3,1,2,0:T(8,128)(2,1)} copy(bf16[4,1024,6,128]{1,0,3,2:T(4,128)(2,1)} %reshape.82) | data formatting | bytes 12582912
  335.7 143.7 %while.15 = (s32[]{:T(128)}, f32[6,1024]{1,0:T(8,128)S(1)}, f32[6,1024]{1,0:T(8,128)S(1)}, f32[6,1024,128]{2,1,0:T(8,128)}, bf16[4,1024,6,128]{3,1,2,0:T(8,128)(...) while((s32[]{:T(128)}, f32[6,1024]{1,0:T(8,128)S(1)}, ...), condition=%wide.region_9.10_spmd.clone, body=%wide.region_6.9_spmd.clone.sunk | while | flops 3273947136 | bytes 86901856 | solution.py:91
  335.7 11.5 %bitcast_reduce_fusion.2 = (f32[6,1024]{1,0:T(8,128)S(1)}, f32[6,1024,1024]{2,1,0:T(8,128)}) fusion(bf16[6,1024,128]{2,1,0:T(8,128)(2,1)S(1)} %get-tuple-element.195, bf16[4,1024,6,128]{3,1,2,0:T(8,128)(2,1)} %get-tuple-element.194, s32[]{:T(128)} %get-tuple-element.181), kind=kOutput, calls=%fused_computation.1.clone.1 | convolution fusion | flops 1623189504 | bytes 28336640 | tf_op jit(solution)/shard_map/while/body/eval_jaxpr/hqd,khd->hqk/dot_general | solution.py:75
  357.7 14.2 %fusion.45 = f32[6,1024,128]{2,1,0:T(8,128)} fusion(f32[6,1024,128]{2,1,0:T(8,128)} %get-tuple-element.184, f32[6,1024,1024]{2,1,0:T(8,128)} %get-tuple-element.169, f32[6,1024]{1,0:T(8,128)S(1)} %select_maximum_fusion.2, bf16[4,1024,6,128]{3,1,2,0:T(8,128)(2,1)} %get-tuple-element.196, s32[]{:T(128)} %get-tuple-element.181, ...), kind=kOutput, calls=%fused_computation.9.clone.1 | convolution fusion | flops 1631846400 | bytes 33079808 | tf_op jit(solution)/shard_map/while/body/eval_jaxpr/hqk,khd->hqd/dot_general | solution.py:82
  371.9 11.5 %bitcast_reduce_fusion.2 = (f32[6,1024]{1,0:T(8,128)S(1)}, f32[6,1024,1024]{2,1,0:T(8,128)}) fusion(bf16[6,1024,128]{2,1,0:T(8,128)(2,1)S(1)} %get-tuple-element.195, bf16[4,1024,6,128]{3,1,2,0:T(8,128)(2,1)} %get-tuple-element.194, s32[]{:T(128)} %get-tuple-element.181), kind=kOutput, calls=%fused_computation.1.clone.1 | convolution fusion | flops 1623189504 | bytes 28336640 | tf_op jit(solution)/shard_map/while/body/eval_jaxpr/hqd,khd->hqk/dot_general | solution.py:75
  383.4 10.5 %fusion.43 = f32[6,1024]{1,0:T(8,128)S(1)} fusion(f32[6,1024,1024]{2,1,0:T(8,128)} %get-tuple-element.169, f32[6,1024]{1,0:T(8,128)S(1)} %select_maximum_fusion.2), kind=kLoop, calls=%fused_computation.4.clone.1 | loop fusion | flops 18868224 | bytes 25214976 | tf_op jit(solution)/shard_map/while/body/eval_jaxpr/reduce_sum | solution.py:81
  394.0 13.7 %fusion.45 = f32[6,1024,128]{2,1,0:T(8,128)} fusion(f32[6,1024,128]{2,1,0:T(8,128)} %get-tuple-element.184, f32[6,1024,1024]{2,1,0:T(8,128)} %get-tuple-element.169, f32[6,1024]{1,0:T(8,128)S(1)} %select_maximum_fusion.2, bf16[4,1024,6,128]{3,1,2,0:T(8,128)(2,1)} %get-tuple-element.196, s32[]{:T(128)} %get-tuple-element.181, ...), kind=kOutput, calls=%fused_computation.9.clone.1 | convolution fusion | flops 1631846400 | bytes 33079808 | tf_op jit(solution)/shard_map/while/body/eval_jaxpr/hqk,khd->hqd/dot_general | solution.py:82
  407.8 11.5 %bitcast_reduce_fusion.2 = (f32[6,1024]{1,0:T(8,128)S(1)}, f32[6,1024,1024]{2,1,0:T(8,128)}) fusion(bf16[6,1024,128]{2,1,0:T(8,128)(2,1)S(1)} %get-tuple-element.195, bf16[4,1024,6,128]{3,1,2,0:T(8,128)(2,1)} %get-tuple-element.194, s32[]{:T(128)} %get-tuple-element.181), kind=kOutput, calls=%fused_computation.1.clone.1 | convolution fusion | flops 1623189504 | bytes 28336640 | tf_op jit(solution)/shard_map/while/body/eval_jaxpr/hqd,khd->hqk/dot_general | solution.py:75
  419.2 10.5 %fusion.43 = f32[6,1024]{1,0:T(8,128)S(1)} fusion(f32[6,1024,1024]{2,1,0:T(8,128)} %get-tuple-element.169, f32[6,1024]{1,0:T(8,128)S(1)} %select_maximum_fusion.2), kind=kLoop, calls=%fused_computation.4.clone.1 | loop fusion | flops 18868224 | bytes 25214976 | tf_op jit(solution)/shard_map/while/body/eval_jaxpr/reduce_sum | solution.py:81
  429.8 13.7 %fusion.45 = f32[6,1024,128]{2,1,0:T(8,128)} fusion(f32[6,1024,128]{2,1,0:T(8,128)} %get-tuple-element.184, f32[6,1024,1024]{2,1,0:T(8,128)} %get-tuple-element.169, f32[6,1024]{1,0:T(8,128)S(1)} %select_maximum_fusion.2, bf16[4,1024,6,128]{3,1,2,0:T(8,128)(2,1)} %get-tuple-element.196, s32[]{:T(128)} %get-tuple-element.181, ...), kind=kOutput, calls=%fused_computation.9.clone.1 | convolution fusion | flops 1631846400 | bytes 33079808 | tf_op jit(solution)/shard_map/while/body/eval_jaxpr/hqk,khd->hqd/dot_general | solution.py:82
  443.6 11.5 %bitcast_reduce_fusion.2 = (f32[6,1024]{1,0:T(8,128)S(1)}, f32[6,1024,1024]{2,1,0:T(8,128)}) fusion(bf16[6,1024,128]{2,1,0:T(8,128)(2,1)S(1)} %get-tuple-element.195, bf16[4,1024,6,128]{3,1,2,0:T(8,128)(2,1)} %get-tuple-element.194, s32[]{:T(128)} %get-tuple-element.181), kind=kOutput, calls=%fused_computation.1.clone.1 | convolution fusion | flops 1623189504 | bytes 28336640 | tf_op jit(solution)/shard_map/while/body/eval_jaxpr/hqd,khd->hqk/dot_general | solution.py:75
  455.1 10.5 %fusion.43 = f32[6,1024]{1,0:T(8,128)S(1)} fusion(f32[6,1024,1024]{2,1,0:T(8,128)} %get-tuple-element.169, f32[6,1024]{1,0:T(8,128)S(1)} %select_maximum_fusion.2), kind=kLoop, calls=%fused_computation.4.clone.1 | loop fusion | flops 18868224 | bytes 25214976 | tf_op jit(solution)/shard_map/while/body/eval_jaxpr/reduce_sum | solution.py:81
  465.6 13.7 %fusion.45 = f32[6,1024,128]{2,1,0:T(8,128)} fusion(f32[6,1024,128]{2,1,0:T(8,128)} %get-tuple-element.184, f32[6,1024,1024]{2,1,0:T(8,128)} %get-tuple-element.169, f32[6,1024]{1,0:T(8,128)S(1)} %select_maximum_fusion.2, bf16[4,1024,6,128]{3,1,2,0:T(8,128)(2,1)} %get-tuple-element.196, s32[]{:T(128)} %get-tuple-element.181, ...), kind=kOutput, calls=%fused_computation.9.clone.1 | convolution fusion | flops 1631846400 | bytes 33079808 | tf_op jit(solution)/shard_map/while/body/eval_jaxpr/hqk,khd->hqd/dot_general | solution.py:82
  479.4 15.5 %bitcast_convert_fusion = bf16[1024,6144]{1,0:T(8,128)(2,1)} fusion(bf16[6,128,6144]{2,1,0:T(8,128)(2,1)} %all-gather.10.cloned.1.call-done, f32[6,1024,128]{2,1,0:T(8,128)} %get-tuple-element.43, f32[6,1024]{1,0:T(8,128)S(1)} %get-tuple-element.44), kind=kOutput, calls=%fused_computation.25 | convolution fusion | flops 9671540736 | bytes 25190400 | tf_op jit(solution)/shard_map/dot_general | solution.py:99
  494.9 129.6 %reduce-scatter.2.cloned.1.call-done = bf16[128,6144]{1,0:T(8,128)(2,1)} async-done(((bf16[1024,6144]{1,0:T(8,128)(2,1)}), bf16[128,6144]{1,0:T(8,128)(2,1)}) %reduce-scatter.2.cloned.1.call-update) | async-done | bytes 1572880 | tf_op jit(solution)/shard_map/reduce_scatter | solution.py:98
  (52 shorter events, 33.0 us)
Async XLA Ops:
  6.5 85.3 %all-gather.6.cloned.1.call-start = ((), (), s32[]{:S(2)}) async-start(), calls=%async_computation.1 | async-start | bytes 1769472 | tf_op jit(solution)/shard_map/all_gather | solution.py:39
  7.3 233.8 %all-gather.8.cloned.1.call-start = ((), (), s32[]{:S(2)}) async-start(), calls=%async_computation.2 | async-start | bytes 7864320 | tf_op jit(solution)/shard_map/all_gather | solution.py:63
  8.0 36.8 %copy-start.1 = (bf16[6144]{0:T(1024)(128)(2,1)S(1)}, bf16[6144]{0:T(1024)(128)(2,1)}, u32[]{:S(2)}) copy-start(bf16[6144]{0:T(1024)(128)(2,1)} %param.12) | copy-start | bytes 36868
  8.0 36.8 %copy-start.2 = (f32[2,6,128]{2,0,1:T(2,128)S(1)}, f32[2,6,128]{2,0,1:T(2,128)}, u32[]{:S(2)}) copy-start(f32[2,6,128]{2,0,1:T(2,128)} %param.14) | copy-start | bytes 18436
  162.7 3.6 copy-start
  168.1 144.8 %all-gather.12.cloned.1.call-start = ((), (), s32[]{:S(2)}) async-start(), calls=%async_computation.5 | async-start | bytes 7864320 | tf_op jit(solution)/shard_map/all_gather | solution.py:64
  171.5 307.9 %all-gather.10.cloned.1.call-start = ((), (), s32[]{:S(2)}) async-start(), calls=%async_computation.3 | async-start | bytes 11796480 | tf_op jit(solution)/shard_map/all_gather | solution.py:95
  172.1 452.4 %reduce-scatter.2.cloned.1.call-start = ((), (), s32[]{:S(2)}) async-start(), calls=%async_computation.4 | async-start | bytes 14155776 | tf_op jit(solution)/shard_map/reduce_scatter | solution.py:98
Sparse Core Ops, SparseCore 0:
  8.9 27.9 all-gather.5
  168.2 72.7 all-gather.7
  242.9 70.0 all-gather.11
  314.7 96.2 all-gather.9
  495.0 129.3 reduce-scatter.1
where the time goes:
time: 634 us; the launch traced here: 631 us
  waiting for transfers between devices  248 us (39%)
  matrix products  177 us (28%)
  other arithmetic  104 us (16%)
  local copies, waits for them, and re-layouts  88.6 us (14%)
  between operations  13.3 us (2%)
    reduce_scatter x1, waiting for transfers between devices, local(): lax.psum_scatter(jnp.dot(context, out_weight, preferred_element_type=jnp....  130 us
    all_gather x1, waiting for transfers between devices, local(): key_piece = lax.all_gather(keys_here, 'row', axis=0, tiled=True)  67.7 us
    unnamed x10, local copies, waits for them, and re-layouts  62.5 us
    dot_general x4, matrix products, step_block(): jnp.einsum('hqk,khd->hqd', exponent.astype(jnp.bfloat16), block_values, p...  55.5 us
    all_gather x1, waiting for transfers between devices, local(): value_piece = lax.all_gather(values_here, 'row', axis=0, tiled=True)  49.2 us
    sin x1, other arithmetic, sincos_table(): jnp.sin(row_angle)  46.9 us
    dot_general x4, matrix products, step_block(): jnp.einsum('hqd,khd->hqk', query_heads, block_keys, preferred_element_typ...  45.9 us
    reduce_sum x4, other arithmetic, step_block(): new_total = run_total * rescale + jnp.sum(exponent, axis=2)  42.2 us
  transfers between devices with their start and end apart: 5, of which 3 were waited for; matrix products, arithmetic and copies ran while one was open for 44% of the time, Pallas kernels for 0%

commit v1 on v0

v1 whole, which is shorter than its diff:
```python
import functools
import math

import jax
import jax.numpy as jnp
from jax import lax
from jax.experimental import pallas as pl
from jax.experimental.pallas import tpu as pltpu
from jax.sharding import PartitionSpec as P

NORM_EPS = 1e-06
KEY_BLOCK = 1024
CHUNKS = 4


def sincos_half(ids, model_width):
    quarter = model_width // 4
    frequency = 1.0 / 10000.0 ** (jnp.arange(quarter, dtype=jnp.float32) / quarter)
    angle = ids.astype(jnp.float32)[:, None] * frequency[None, :]
    return jnp.concatenate([jnp.sin(angle), jnp.cos(angle)], axis=1)


def layer_norm(values, gain_row):
    mean_val = jnp.mean(values, axis=-1, keepdims=True)
    centered = values - mean_val
    variance = jnp.mean(centered * centered, axis=-1, keepdims=True)
    return centered * lax.rsqrt(variance + NORM_EPS) * gain_row


def attention_kernel(key_block, exp_factor, q_ref, k_ref, v_ref, out_ref):
    rows, head_size = math.prod(q_ref.shape[:-1]), q_ref.shape[-1]
    query = q_ref[...].reshape(rows, head_size)
    peak = jnp.full((rows, 1), -1e30, jnp.float32)
    total = jnp.zeros((rows, 1), jnp.float32)
    acc = jnp.zeros((rows, head_size), jnp.float32)
    for start in range(0, k_ref.shape[0], key_block):
        scores = lax.dot_general(
            query,
            k_ref[start : start + key_block, :],
            (((1,), (1,)), ((), ())),
            preferred_element_type=jnp.float32,
        )
        new_peak = jnp.maximum(peak, jnp.max(scores, axis=1, keepdims=True) * exp_factor)
        rescale = jnp.exp2(peak - new_peak)
        weights = jnp.exp2(scores * exp_factor - new_peak)
        total = total * rescale + jnp.sum(weights, axis=1, keepdims=True)
        acc = acc * rescale + jnp.dot(
            weights.astype(jnp.bfloat16),
            v_ref[start : start + key_block, :],
            preferred_element_type=jnp.float32,
        )
        peak = new_peak
    out_ref[...] = (acc / total).astype(out_ref.dtype).reshape(out_ref.shape)


def attention(queries, keys_values, chunk, chunk_rows, width, head_size):
    owners = queries.shape[0]
    heads = width // head_size
    key_count = keys_values.shape[0]
    key_block = math.gcd(key_count, KEY_BLOCK)
    exp_factor = math.log2(math.e) / math.sqrt(head_size)
    rows = owners * chunk_rows
    elements = heads * rows * key_count
    return pl.pallas_call(
        functools.partial(attention_kernel, key_block, exp_factor),
        grid=(heads,),
        in_specs=[
            pl.BlockSpec((owners, chunk_rows, head_size), lambda h: (0, chunk, h)),
            pl.BlockSpec((key_count, head_size), lambda h: (0, h)),
            pl.BlockSpec((key_count, head_size), lambda h: (0, heads + h)),
        ],
        out_specs=pl.BlockSpec((owners, chunk_rows, head_size), lambda h: (0, 0, h)),
        out_shape=jax.ShapeDtypeStruct((owners, chunk_rows, width), jnp.bfloat16),
        compiler_params=pltpu.CompilerParams(
            dimension_semantics=("arbitrary",),
            vmem_limit_bytes=48 * 1024 * 1024,
        ),
        cost_estimate=pl.CostEstimate(
            flops=4 * elements * head_size,
            bytes_accessed=4 * (rows + key_count) * width,
            transcendentals=elements,
        ),
        name="attention",
    )(queries, keys_values, keys_values)


def norm_kernel(x_ref, gain_ref, out_ref):
    out_ref[...] = layer_norm(x_ref[...], gain_ref[...]).astype(out_ref.dtype)


def norm_heads(projected, gain_row, head_size):
    rows, width = projected.shape[0], gain_row.shape[1]
    return pl.pallas_call(
        norm_kernel,
        grid=(width // head_size,),
        in_specs=[
            pl.BlockSpec((rows, head_size), lambda h: (0, h)),
            pl.BlockSpec((1, head_size), lambda h: (0, h)),
        ],
        out_specs=pl.BlockSpec((rows, head_size), lambda h: (0, h)),
        out_shape=jax.ShapeDtypeStruct((rows, width), jnp.bfloat16),
        compiler_params=pltpu.CompilerParams(dimension_semantics=("arbitrary",)),
        cost_estimate=pl.CostEstimate(
            flops=10 * rows * width, bytes_accessed=6 * rows * width, transcendentals=rows
        ),
        name="norm_heads",
    )(projected, gain_row)


def local(patches, w_patch, patch_bias, ln_gain, w_qkv, qk_gain, w_out):
    tile_rows, tile_cols, pixel_width = patches.shape
    model_width = w_patch.shape[1]
    heads_here = w_qkv.shape[2]
    head_size = w_qkv.shape[3]
    col_count = lax.axis_size("col")
    block_tokens = tile_rows * tile_cols * col_count
    row_anchor = lax.axis_index("row") * tile_rows
    qkv_matrix = w_qkv.reshape(model_width, 3 * heads_here * head_size)
    bias_row = patch_bias.astype(jnp.float32)[None, :]
    gain_row = ln_gain.astype(jnp.float32)
    pixels = lax.all_gather(patches, "col", axis=1, tiled=True)
    piece_cols = pixels.shape[1]
    flat_pixels = pixels.reshape(tile_rows * piece_cols, pixel_width)
    embedded = jnp.dot(flat_pixels, w_patch, preferred_element_type=jnp.float32) + bias_row
    row_half = sincos_half(row_anchor + jnp.arange(tile_rows, dtype=jnp.int32), model_width)
    col_half = sincos_half(jnp.arange(piece_cols, dtype=jnp.int32), model_width)
    row_half, col_half = lax.optimization_barrier((row_half, col_half))
    half_shape = (tile_rows, piece_cols, model_width // 2)
    position = jnp.concatenate(
        [
            jnp.broadcast_to(row_half[:, None, :], half_shape),
            jnp.broadcast_to(col_half[None, :, :], half_shape),
        ],
        axis=2,
    )
    embedded = embedded + position.reshape(tile_rows * piece_cols, model_width)
    normed = layer_norm(embedded, gain_row).astype(jnp.bfloat16)
    normed_piece = normed.reshape(tile_rows, piece_cols, model_width)
    project_piece_cols = normed_piece.shape[1]
    flat_normed = normed_piece.reshape(tile_rows * project_piece_cols, model_width)
    projected = jnp.dot(flat_normed, qkv_matrix, preferred_element_type=jnp.float32)
    head_width = heads_here * head_size
    gain_qk = qk_gain.reshape(1, 2 * head_width)
    normed_qk = norm_heads(projected, gain_qk, head_size)
    keys_values = jnp.concatenate(
        [normed_qk[:, head_width:], projected[:, 2 * head_width :].astype(jnp.bfloat16)], axis=1
    )
    keys_values = lax.all_gather(keys_values, "row", axis=0, tiled=True)
    out_weight = lax.all_gather(w_out, "row", axis=2, tiled=True).reshape(
        heads_here * head_size, model_width
    )
    owned = block_tokens // col_count
    chunk_rows = owned // math.gcd(owned // 16, CHUNKS)
    queries = normed_qk.reshape(col_count, owned, 2 * head_width)
    pieces = []
    for chunk in range(owned // chunk_rows):
        context = attention(queries, keys_values, chunk, chunk_rows, head_width, head_size)
        partial = jnp.dot(
            context.reshape(col_count * chunk_rows, head_width),
            out_weight,
            preferred_element_type=jnp.float32,
        ).astype(jnp.bfloat16)
        pieces.append(lax.psum_scatter(partial, "col", scatter_dimension=0, tiled=True))
    return jnp.concatenate(pieces, axis=0)


def solution(mesh):
    return jax.shard_map(
        local,
        mesh=mesh,
        in_specs=(
            P("row", "col", None),
            P(),
            P(),
            P(),
            P(None, None, "col", None),
            P(None, "col", None),
            P("col", None, "row"),
        ),
        out_specs=P(("row", "col"), None),
        check_vma=False,
    )
```

time: 634 us -> 563 us (0.89)
  matrix products: 177 us -> 95.3 us
  other arithmetic: 104 us -> 31.3 us
  Pallas kernels: 0 us -> 66.9 us
  waiting for transfers between devices: 248 us -> 309 us
  local copies, waits for them, and re-layouts: 88.6 us -> 45.6 us
    dot_general x9 -> x4, matrix products: 117 us -> 31 us  [local(): jnp.dot(context.reshape(col_count * chunk_rows, head_width), out_weight,...]
    all_gather x1, waiting for transfers between devices: 0.01 us -> 84.1 us  [local(): lax.all_gather(w_out, 'row', axis=2, tiled=True)]
    pallas_call x0 -> x5, Pallas kernels: none -> 66.9 us  [the longest x4 56.5 us: attention(): pl.pallas_call(functools.partial(attention_kernel, key_block, exp_factor)...]
    sin x1 -> x2, other arithmetic: 46.9 us -> 3.04 us  [sincos_half(): return jnp.concatenate([jnp.sin(angle), jnp.cos(angle)], axis=1)]
    reduce_sum x5 -> x0, other arithmetic: 42.9 us -> none  [the longest x4 42.2 us: step_block(): new_total = run_total * rescale + jnp.sum(exponent, axis=2)]
    reduce_scatter x1 -> x4, waiting for transfers between devices: 130 us -> 100 us  [local(): lax.psum_scatter(partial, 'col', scatter_dimension=0, tiled=True)]
    unnamed x10 -> x8, local copies, waits for them, and re-layouts: 62.5 us -> 37 us
    reshape x2 -> x1, local copies, waits for them, and re-layouts: 22.7 us -> 0.6 us  [local(): gain_qk = qk_gain.reshape(1, 2 * head_width)]
  transfers between devices with their start and end apart: 5 -> 7, of which waited for: 3 -> 5; matrix products, arithmetic and copies ran while one was open for 44% -> 14% of each run, Pallas kernels for 0% -> 10%
where the time goes in v1:
time: 563 us; the launch traced here: 562 us
  waiting for transfers between devices  309 us (55%)
  matrix products  95.3 us (17%)
  Pallas kernels  66.9 us (12%)
  local copies, waits for them, and re-layouts  45.6 us (8%)
  other arithmetic  31.3 us (6%)
  between operations  13.6 us (2%)
    all_gather x1, waiting for transfers between devices, local(): keys_values = lax.all_gather(keys_values, 'row', axis=0, tiled=True)  123 us
    reduce_scatter x4, waiting for transfers between devices, local(): lax.psum_scatter(partial, 'col', scatter_dimension=0, tiled=True)  100 us
    all_gather x1, waiting for transfers between devices, local(): lax.all_gather(w_out, 'row', axis=2, tiled=True)  84.1 us
    pallas_call x4, Pallas kernels, attention(): pl.pallas_call(functools.partial(attention_kernel, key_block, exp_factor)...  56.5 us
    dot_general x1, matrix products, local(): jnp.dot(flat_normed, qkv_matrix, preferred_element_type=jnp.float32)  39 us
    unnamed x8, local copies, waits for them, and re-layouts  37 us
    dot_general x4, matrix products, local(): jnp.dot(context.reshape(col_count * chunk_rows, head_width), out_weight,...  31 us
    dot_general x1, matrix products, local(): jnp.dot(flat_pixels, w_patch, preferred_element_type=jnp.float32) + bias_row  25.3 us
  transfers between devices with their start and end apart: 7, of which 5 were waited for; matrix products, arithmetic and copies ran while one was open for 14% of the time, Pallas kernels for 10%

profile of v1, /device:TPU:0, one launch (start us, length us, event | category | flops | bytes accessed | tf_op | source)
XLA Modules:
  0.0 561.8 jit_solution(9421970326799950756)
XLA Ops:
  7.6 2.8 multiply_sine_fusion
  11.2 37.0 %copy.9 = bf16[6144,3,6,128]{0,3,2,1:T(8,128)(2,1)} copy(bf16[6144,3,6,128]{3,0,2,1:T(8,128)(2,1)} %param.11) | data formatting | bytes 56623104 | tf_op args[4]
  52.0 11.2 %pad_maximum_fusion = f32[8,128,6144]{2,1,0:T(8,128)} fusion(f32[8,128,3072]{2,1,0:T(8,128)S(1)} %broadcast_in_dim.5, f32[8,128,3072]{2,1,0:T(8,128)S(1)} %broadcast_in_dim.4), kind=kLoop, calls=%fused_computation | loop fusion | flops 6291456 | bytes 50331648 | tf_op jit(solution)/shard_map/concatenate | solution.py:129
  63.2 25.3 %fusion.4 = (f32[1024]{0:T(1024)S(1)}, f32[1024,6144]{1,0:T(8,128)}) fusion(f32[8,128,6144]{2,1,0:T(8,128)} %pad_maximum_fusion, f32[6144]{0:T(1024)S(1)} %convert_element_type.38, bf16[1024,768]{1,0:T(8,128)(2,1)} %bitcast.34, bf16[768,6144]{1,0:T(8,128)(2,1)} %param.8), kind=kOutput, calls=%fused_computation.26 | convolution fusion | flops 9682549760 | bytes 61370368 | tf_op jit(solution)/shard_map/dot_general | solution.py:124
  88.5 10.2 %multiply_reduce_fusion = f32[1024]{0:T(1024)S(1)} fusion(f32[1024,6144]{1,0:T(8,128)} %get-tuple-element.14, f32[1024]{0:T(1024)S(1)} %broadcast_multiply_fusion), kind=kLoop, calls=%fused_computation.3 | loop fusion | flops 18873344 | bytes 25174016 | tf_op jit(solution)/shard_map/reduce_sum | solution.py:26
  98.7 39.0 %fusion.x_ref = f32[1024,2304]{1,0:T(8,128)} fusion(bf16[6144,2304]{0,1:T(8,128)(2,1)} %bitcast.29, f32[1024,6144]{1,0:T(8,128)} %get-tuple-element.14, f32[6144]{0:T(1024)S(1)} %convert_element_type.41, f32[1024]{0:T(1024)S(1)} %add_rsqrt_fusion, f32[1024]{0:T(1024)S(1)} %broadcast_multiply_fusion), kind=kOutput, calls=%fused_computation.4 | convolution fusion | flops 29016195072 | bytes 62947328 | tf_op jit(solution)/shard_map/dot_general | solution.py:141
  137.7 3.2 slice.12
  140.9 10.5 %norm_heads.1 = bf16[1024,1536]{1,0:T(8,128)(2,1)} custom-call(f32[1024,2304]{1,0:T(8,128)} %fusion.x_ref, f32[1,1536]{1,0:T(1,128)} %reshape.64.gain_ref), custom_call_target="tpu_custom_call" | custom-call | flops 15728640 | bytes 9437184 | tf_op jit(solution)/shard_map/norm_heads/pallas_call | solution.py:93
  151.4 1.7 slice.9
  153.1 3.4 pad_maximum_fusion.1
  157.2 123.0 %all-gather.6.cloned.1.call-done.k_ref.v_ref = bf16[4096,1536]{1,0:T(8,128)(2,1)} async-done(((bf16[1024,1536]{1,0:T(8,128)(2,1)}), bf16[4096,1536]{1,0:T(8,128)(2,1)}) %all-gather.6.cloned.1.call-update) | async-done | bytes 12582928 | tf_op jit(solution)/shard_map/all_gather | solution.py:148
  280.2 14.0 %attention.4 = bf16[8,32,768]{2,1,0:T(8,128)(2,1)S(1)} custom-call(bf16[8,128,1536]{2,1,0:T(8,128)(2,1)S(1)} %bitcast.21, bf16[4096,1536]{1,0:T(8,128)(2,1)} %all-gather.6.cloned.1.call-done.k_ref.v_ref, bf16[4096,1536]{1,0:T(8,128)(2,1)} %all-gather.6.cloned.1.call-done.k_ref.v_ref), custom_call_target="tpu_custom_call" | custom-call | flops 3221225472 | bytes 13369344 | tf_op jit(solution)/shard_map/attention/pallas_call | solution.py:64
  294.3 84.1 %all-gather.8.cloned.1.call-done = bf16[6,128,6144]{2,1,0:T(8,128)(2,1)} async-done(((bf16[6,128,1536]{2,1,0:T(8,128)(2,1)}), bf16[6,128,6144]{2,1,0:T(8,128)(2,1)}) %all-gather.8.cloned.1.call-update) | async-done | bytes 9437200 | tf_op jit(solution)/shard_map/all_gather | solution.py:149
  378.3 7.7 %convolution_convert_fusion.3 = bf16[256,6144]{1,0:T(8,128)(2,1)} fusion(bf16[256,768]{1,0:T(8,128)(2,1)S(1)} %bitcast.25, bf16[768,6144]{1,0:T(8,128)(2,1)} %bitcast.30), kind=kOutput, calls=%fused_computation.11 | convolution fusion | flops 2417491968 | bytes 12976128 | tf_op jit(solution)/shard_map/dot_general | solution.py:158
  386.1 14.0 %attention.5 = bf16[8,32,768]{2,1,0:T(8,128)(2,1)S(1)} custom-call(bf16[8,128,1536]{2,1,0:T(8,128)(2,1)S(1)} %bitcast.22, bf16[4096,1536]{1,0:T(8,128)(2,1)} %all-gather.6.cloned.1.call-done.k_ref.v_ref, bf16[4096,1536]{1,0:T(8,128)(2,1)} %all-gather.6.cloned.1.call-done.k_ref.v_ref), custom_call_target="tpu_custom_call" | custom-call | flops 3221225472 | bytes 13369344 | tf_op jit(solution)/shard_map/attention/pallas_call | solution.py:64
  400.1 7.8 %convolution_convert_fusion.2 = bf16[256,6144]{1,0:T(8,128)(2,1)} fusion(bf16[256,768]{1,0:T(8,128)(2,1)S(1)} %bitcast.27, bf16[768,6144]{1,0:T(8,128)(2,1)} %bitcast.31), kind=kOutput, calls=%fused_computation.10 | convolution fusion | flops 2417491968 | bytes 12976128 | tf_op jit(solution)/shard_map/dot_general | solution.py:158
  408.0 14.1 %attention.6 = bf16[8,32,768]{2,1,0:T(8,128)(2,1)S(1)} custom-call(bf16[8,128,1536]{2,1,0:T(8,128)(2,1)S(1)} %bitcast.23, bf16[4096,1536]{1,0:T(8,128)(2,1)} %all-gather.6.cloned.1.call-done.k_ref.v_ref, bf16[4096,1536]{1,0:T(8,128)(2,1)} %all-gather.6.cloned.1.call-done.k_ref.v_ref), custom_call_target="tpu_custom_call" | custom-call | flops 3221225472 | bytes 13369344 | tf_op jit(solution)/shard_map/attention/pallas_call | solution.py:64
  422.0 7.7 %convolution_convert_fusion.1 = bf16[256,6144]{1,0:T(8,128)(2,1)} fusion(bf16[256,768]{1,0:T(8,128)(2,1)S(1)} %bitcast.28, bf16[768,6144]{1,0:T(8,128)(2,1)} %bitcast.32), kind=kOutput, calls=%fused_computation.9 | convolution fusion | flops 2417491968 | bytes 12976128 | tf_op jit(solution)/shard_map/dot_general | solution.py:158
  429.9 14.3 %attention.7 = bf16[8,32,768]{2,1,0:T(8,128)(2,1)S(1)} custom-call(bf16[8,128,1536]{2,1,0:T(8,128)(2,1)S(1)} %bitcast.24, bf16[4096,1536]{1,0:T(8,128)(2,1)} %all-gather.6.cloned.1.call-done.k_ref.v_ref, bf16[4096,1536]{1,0:T(8,128)(2,1)} %all-gather.6.cloned.1.call-done.k_ref.v_ref), custom_call_target="tpu_custom_call" | custom-call | flops 3221225472 | bytes 13369344 | tf_op jit(solution)/shard_map/attention/pallas_call | solution.py:64
  444.2 7.8 %convolution_convert_fusion = bf16[256,6144]{1,0:T(8,128)(2,1)} fusion(bf16[256,768]{1,0:T(8,128)(2,1)S(1)} %bitcast.26, bf16[768,6144]{1,0:T(8,128)(2,1)} %bitcast.33), kind=kOutput, calls=%fused_computation.8 | convolution fusion | flops 2417491968 | bytes 12976128 | tf_op jit(solution)/shard_map/dot_general | solution.py:158
  452.0 16.3 %reduce-scatter.7.cloned.1.call-done = bf16[32,6144]{1,0:T(8,128)(2,1)} async-done(((bf16[256,6144]{1,0:T(8,128)(2,1)}), bf16[32,6144]{1,0:T(8,128)(2,1)}) %reduce-scatter.7.cloned.1.call-update) | async-done | bytes 393232 | tf_op jit(solution)/shard_map/reduce_scatter | solution.py:163
  468.3 41.8 %reduce-scatter.9.cloned.1.call-done = bf16[32,6144]{1,0:T(8,128)(2,1)} async-done(((bf16[256,6144]{1,0:T(8,128)(2,1)}), bf16[32,6144]{1,0:T(8,128)(2,1)}) %reduce-scatter.9.cloned.1.call-update) | async-done | bytes 393232 | tf_op jit(solution)/shard_map/reduce_scatter | solution.py:163
  510.2 42.1 %reduce-scatter.11.cloned.1.call-done = bf16[32,6144]{1,0:T(8,128)(2,1)} async-done(((bf16[256,6144]{1,0:T(8,128)(2,1)}), bf16[32,6144]{1,0:T(8,128)(2,1)}) %reduce-scatter.11.cloned.1.call-update) | async-done | bytes 393232 | tf_op jit(solution)/shard_map/reduce_scatter | solution.py:163
  552.3 2.6 pad_maximum_fusion.3
  (36 shorter events, 6.6 us)
Async XLA Ops:
  6.5 56.7 %all-gather.4.cloned.1.call-start = ((), (), s32[]{:S(2)}) async-start(), calls=%async_computation.4 | async-start | bytes 1769472 | tf_op jit(solution)/shard_map/all_gather | solution.py:121
  7.3 273.0 %all-gather.6.cloned.1.call-start = ((), (), s32[]{:S(2)}) async-start(), calls=%async_computation.5 | async-start | bytes 15728640 | tf_op jit(solution)/shard_map/all_gather | solution.py:148
  11.2 37.0 %copy-start.1 = (bf16[6144]{0:T(1024)(128)(2,1)S(1)}, bf16[6144]{0:T(1024)(128)(2,1)}, u32[]{:S(2)}) copy-start(bf16[6144]{0:T(1024)(128)(2,1)} %param.10) | copy-start | bytes 36868
  11.2 37.0 %copy-start.2 = (f32[2,6,128]{2,0,1:T(2,128)S(1)}, f32[2,6,128]{2,0,1:T(2,128)}, u32[]{:S(2)}) copy-start(f32[2,6,128]{2,0,1:T(2,128)} %param.12) | copy-start | bytes 18436
  151.4 128.9 %copy-start = (bf16[1024,1536]{1,0:T(8,128)(2,1)S(1)}, bf16[1024,1536]{1,0:T(8,128)(2,1)}, u32[]{:S(2)}) copy-start(bf16[1024,1536]{1,0:T(8,128)(2,1)} %norm_heads.1) | copy-start | bytes 9437188
  156.4 221.9 %all-gather.8.cloned.1.call-start = ((), (), s32[]{:S(2)}) async-start(), calls=%async_computation.6 | async-start | bytes 11796480 | tf_op jit(solution)/shard_map/all_gather | solution.py:149
  157.2 294.8 %reduce-scatter.5.cloned.1.call-start = ((), (), s32[]{:S(2)}) async-start(), calls=%async_computation.7 | async-start | bytes 3538944 | tf_op jit(solution)/shard_map/reduce_scatter | solution.py:163
  386.0 82.3 %reduce-scatter.7.cloned.1.call-start = ((), (), s32[]{:S(2)}) async-start(), calls=%async_computation.8 | async-start | bytes 3538944 | tf_op jit(solution)/shard_map/reduce_scatter | solution.py:163
  407.9 102.3 %reduce-scatter.9.cloned.1.call-start = ((), (), s32[]{:S(2)}) async-start(), calls=%async_computation.9 | async-start | bytes 3538944 | tf_op jit(solution)/shard_map/reduce_scatter | solution.py:163
  429.8 122.5 %reduce-scatter.11.cloned.1.call-start = ((), (), s32[]{:S(2)}) async-start(), calls=%async_computation.10 | async-start | bytes 3538944 | tf_op jit(solution)/shard_map/reduce_scatter | solution.py:163
Sparse Core Ops, SparseCore 0:
  8.9 27.9 all-gather.3
  156.6 123.6 all-gather.5
  282.1 96.1 all-gather.7
  386.1 40.3 reduce-scatter.4
  428.7 39.6 reduce-scatter.6
  470.5 39.6 reduce-scatter.8
  512.5 39.7 reduce-scatter.10
